TPU v7x, 32 devices: a whole 2x2x4 slice. The times are simulated.
32 devices in a mesh: srow: 4 (over y, core), scol: 8 (over z, x).
Axes of the slice: x: 2, y: 2, z: 4, core: 2. Of those that a mesh axis runs over, the one named last changes fastest.
Arguments:
- loads: float32 [4, 16, 4, 128], P('srow', 'scol'), may hold values from -6 to 6
- local_inverse: float32 [4, 16, 128, 128], P('srow', 'scol'), as said below
- dirichlet: float32 [4, 16, 128, 128], P('srow', 'scol'), as said below
- corner_coupling: float32 [4, 16, 128], P('srow', 'scol'), may hold values from -4 to 4
- coarse_inverse: float32 [4, 16, 16], P('srow', 'scol'), as said below
- partner: int32 [4, 16, 128], P('srow', 'scol'), may hold values from -1 to 31, as said below
Outputs:
- multipliers: float32 [4, 16, 4, 128], P('srow', 'scol')
- residual: float32 [4, 16, 4, 128], P('srow', 'scol')
Inputs may be any that keep to these rules, and one draw needn't show every extreme that they name: `partner`: on each edge of each subdomain the first n entries, for some n of 1 to 32, are the positions 0 to n - 1 in order or reversed, the rest are -1; the two subdomains sharing an edge have the same n and mutually inverse lists. `local_inverse`: each block is symmetric positive definite. `dirichlet`: each block is symmetric positive definite. `coarse_inverse`: each band's matrix is symmetric positive definite.
All inputs are finite; a program needn't handle non-finite values.
Results may differ from a plain program's by a relative error of at most 0.0003.
Values sent between devices are 32-bit elements; how exact they have to be, the bound alone decides.
A program may use at most 64 MiB of HBM per device.

v0:
```python
import functools

import jax
import jax.numpy as jnp
from jax import lax
from jax.experimental import pallas as pl
from jax.experimental.pallas import tpu as pltpu
from jax.sharding import PartitionSpec as P

ITERS = 3
MESH = pl.DeviceIdType.MESH
precise = lax.Precision.HIGHEST
NEAR = ((0, 0), (0, 1), (0, -1), (1, 0), (-1, 0))
FAR = ((1, 1), (1, -1), (-1, 1), (-1, -1), (2, 0), (-2, 0))
UNROLL = 64


def slot_list(nr, nc):
    near, slots = [], []
    for offsets, out in ((NEAR, near), (FAR, None)):
        for di, dj in offsets:
            off = (di % nr, dj % nc)
            if off not in slots:
                slots.append(off)
                if out is not None:
                    out.append(off)
    return near, slots


def kernel(nr, nc, near, slots, sc, nrhs, loads_in, cpl_in, cinv_in, part_in, linv, dirich, out,
           loads, cpl, cinv, part, lbuf, dbuf, lpair, dpair, loads_n, part_n, cpl_n, dnear, kc, kt, ub, qb,
           local_sem, k_send, k_recv, c_send, c_recv, l_send, l_recv, p_send, p_recv, d_send, d_recv,
           u_send, u_recv, q_send, q_recv):
    rows, width = loads.shape
    edge = width // 4
    ndev = nr * nc
    ncols = nc * sc
    lanes = kt.shape[-1]
    i, j = lax.axis_index("srow"), lax.axis_index("scol")

    def target(di, dj):
        return (lax.rem(i - di + nr, nr), lax.rem(j - dj + nc, nc))

    def others(step):
        if ndev <= UNROLL:
            far_first = sorted(range(1, ndev), key=lambda k: (-min(k // nc, nr - k // nc), min(k % nc, nc - k % nc) % (nc // 2)))
            for k in far_first:
                step(k, k // nc, k % nc)
        else:
            @pl.loop(1, ndev)
            def _(k):
                step(k, lax.div(k, nc), lax.rem(k, nc))

    barrier = pltpu.get_barrier_semaphore()

    def greet(k, di, dj):
        pl.semaphore_signal(barrier, inc=1, device_id=target(di, dj), device_id_type=MESH)

    others(greet)

    fetches = [
        pltpu.make_async_copy(src, dst, local_sem.at[n])
        for n, (src, dst) in enumerate((
            (cinv_in, cinv), (loads_in, loads), (cpl_in, cpl), (part_in, part),
            (linv, lbuf), (dirich, dbuf),
        ))
    ]
    for fetch in fetches:
        fetch.start()

    row = lax.broadcasted_iota(jnp.int32, (rows, width), 0)
    lane = lax.broadcasted_iota(jnp.int32, (rows, width), 1)
    wrow = lax.broadcasted_iota(jnp.int32, (rows, lanes), 0)
    wlane = lax.broadcasted_iota(jnp.int32, (rows, lanes), 1)
    wrhs = lax.rem(wrow, nrhs)
    wsub = lax.div(wrow, nrhs)
    of_rhs = lax.div(wlane, ncols) == wrhs
    gamma_lane = wlane == nrhs * ncols + wrhs
    curve_lane = wlane == nrhs * ncols + nrhs + wrhs

    def spread(block):
        out = jnp.broadcast_to(block[0:1], (rows, block.shape[1]))
        which = lax.div(lax.broadcasted_iota(jnp.int32, out.shape, 0), nrhs)
        for s in range(1, sc):
            out = jnp.where(which == s, jnp.broadcast_to(block[s : s + 1], out.shape), out)
        return out

    def place(dj):
        column = lax.rem(j + dj, nc) * sc
        return wlane == wrhs * ncols + column + wsub

    def index_of(block):
        partner = spread(block)
        position = jnp.clip(partner, 0, edge - 1) + (edge * (1 - 2 * lax.rem(lax.div(lane, edge), 2)) + lax.div(lane, edge) * edge)
        return position, partner >= 0

    def split(values):
        high = values.astype(jnp.bfloat16)
        return high, (values - high.astype(jnp.float32)).astype(jnp.bfloat16)

    def split_into(pair, blocks):
        for s, block in enumerate(blocks):
            high, low = split(block)
            pair[s * width : (s + 1) * width, 0:width] = high
            pair[s * width : (s + 1) * width, width : 2 * width] = low

    tile_lane = lax.broadcasted_iota(jnp.int32, (ncols, lanes), 1)
    tile_row = lax.broadcasted_iota(jnp.int32, (ncols, lanes), 0)
    tiler = jnp.where(lax.rem(tile_lane, ncols) == tile_row, 1.0, 0.0)
    for fetch in fetches[:4]:
        fetch.wait()
    tiled = jnp.dot(spread(cinv[...]), tiler, precision=precise, preferred_element_type=jnp.float32)
    for s in range(sc):
        kc[0, s : s + 1] = tiled[s * nrhs : s * nrhs + 1]
    kt[0] = jnp.where(of_rhs, tiled, 0.0)

    own_position, own_active = index_of(part[...])
    coupling = spread(cpl[...])
    own_place = place(0)
    pl.semaphore_wait(barrier, ndev - 1)

    def remote(src, dst, send, recv, off):
        copy = pltpu.make_async_remote_copy(
            src_ref=src, dst_ref=dst, send_sem=send, recv_sem=recv,
            device_id=target(*off), device_id_type=MESH)
        copy.start()
        return copy

    load_copies = [remote(loads, loads_n.at[n], l_send.at[n], l_recv.at[n], near[n]) for n in range(1, len(near))]
    part_copies = [remote(part, part_n.at[n], p_send.at[n], p_recv.at[n], near[n]) for n in range(1, len(near))]
    fetches[4].wait()
    split_into(lpair, [lbuf[s] for s in range(sc)])
    for n in range(1, len(near)):
        dpair[n] = jnp.zeros(dpair.shape[1:], jnp.bfloat16)

    cpl_copies = [remote(cpl, cpl_n.at[n], c_send.at[n], c_recv.at[n], slots[n]) for n in range(1, len(slots))]
    east_off, west_off = (0, 1 % nc), (0, nc - 1)
    facing_start = {east_off: 0, west_off: edge, (1 % nr, 0): 2 * edge, (nr - 1, 0): 3 * edge}
    d_copies = []
    for n in range(1, len(near)):
        subs = {east_off: pl.ds(0, 1), west_off: pl.ds(sc - 1, 1)}.get(near[n], pl.ds(0, sc))
        src = dirich.at[subs, pl.ds(facing_start[near[n]], edge)]
        d_copies.append((src, dnear.at[n, subs], d_send.at[n], d_recv.at[n], near[n]))

    def send_k(k, di, dj):
        remote(kc.at[0], kc.at[k], k_send, k_recv, (di, dj))

    others(send_k)
    d_copies = [remote(*args) for args in d_copies]

    def jump(mine, west_tile, east_tile, south, north, lookup):
        position, active = lookup
        west = jnp.where(row < nrhs, pltpu.roll(west_tile, nrhs, 0), pltpu.roll(mine, nrhs, 0))
        east = jnp.where(row >= rows - nrhs, pltpu.roll(east_tile, rows - nrhs, 0), pltpu.roll(mine, rows - nrhs, 0))
        side = lax.div(lane, edge)
        comb = jnp.where(side == 0, east, jnp.where(side == 1, west, jnp.where(side == 2, north, south)))
        facing = jnp.take_along_axis(comb, position, axis=1, mode="promise_in_bounds")
        return jnp.where(active, mine - facing, 0.0)

    def slot_of(di, dj):
        off = (di % nr, dj % nc)
        return slots.index(off) if off in slots else None

    def jump_at(tiles, di, dj, lookup):
        def tile(a, b):
            n = slot_of(a, b)
            return tiles[n] if n is not None and n in tiles else tiles[slot_of(di, dj)]
        return jump(tiles[slot_of(di, dj)], tile(di, dj - 1), tile(di, dj + 1), tile(di - 1, dj), tile(di + 1, dj), lookup)

    def multiply(values, pair, count):
        high, low = split(values)
        stacked = jnp.concatenate([high.astype(jnp.float32), low.astype(jnp.float32)], axis=0)
        sub = lax.rem(lax.div(lax.broadcasted_iota(jnp.int32, stacked.shape, 0), nrhs), sc)
        wide = jnp.concatenate(
            [jnp.where(sub == (s if s < count - 1 else sc - 1), stacked, 0.0) for s in range(count)], axis=1)
        product = jnp.dot(wide.astype(jnp.bfloat16), pair, preferred_element_type=jnp.float32)
        return (product[0:rows, 0:width] + product[rows:, 0:width]) + (product[0:rows, width:] + product[rows:, width:])

    def lane_sum(values):
        return jnp.sum(values, axis=1, keepdims=True)

    def publish(rd, values, dots, wide):
        u = multiply(values, lpair[...], sc)
        ub[rd, 0] = u
        count = len(slots) if wide else len(near)
        for n in range(1, count):
            remote(ub.at[rd, 0], ub.at[rd, n], u_send.at[rd], u_recv.at[rd], slots[n])
        message = jnp.where(own_place, lane_sum(coupling * values), 0.0)
        if dots is not None:
            gamma, factor = dots
            message = jnp.where(gamma_lane, lane_sum(gamma), message)
            message = jnp.where(curve_lane, lane_sum(factor * u), message)
        qb[rd, 0] = jnp.sum(message, axis=0, keepdims=True)

        def send_q(k, di, dj):
            remote(qb.at[rd, 0], qb.at[rd, k], q_send.at[rd], q_recv.at[rd], (di, dj))

        others(send_q)
        return count

    def collect(rd, count, want_dots):
        bytes_q = qb.at[rd, pl.ds(1, ndev - 1)]
        pltpu.make_async_copy(bytes_q, bytes_q, q_recv.at[rd]).wait()
        band = [jnp.broadcast_to(jnp.sum(qb[rd, pl.ds(d * nc, nc)], axis=0), (rows, lanes)) for d in range(nr)]
        cols = {}

        def column(k, d):
            return lane_sum(band[d] * kt[k])

        gamma = curve = None
        if want_dots:
            cross = jnp.zeros((rows, lanes), jnp.float32)
            for d in range(nr):
                total = jnp.zeros((rows, lanes), jnp.float32)
                if ndev <= UNROLL:
                    for e in range(nc):
                        cols[(d, e)] = column(d * nc + e, d)
                        total = total + jnp.where(place(e), cols[(d, e)], 0.0)
                else:
                    def add(e, total):
                        return total + jnp.where(place(e), column(d * nc + e, d), 0.0)
                    total = lax.fori_loop(0, nc, add, total)
                cross = cross + total * band[d]
            everything = functools.reduce(jnp.add, band)
            crossed = jnp.broadcast_to(jnp.sum(cross, axis=0, keepdims=True), (rows, lanes))
            curve = lane_sum(jnp.where(of_rhs, crossed, 0.0) + jnp.where(curve_lane, everything, 0.0))
            gamma = lane_sum(jnp.where(gamma_lane, everything, 0.0))
        bytes_u = ub.at[rd, pl.ds(1, count - 1)]
        pltpu.make_async_copy(bytes_u, bytes_u, u_recv.at[rd]).wait()
        tiles = {}
        for n in range(count):
            off = slots[n]
            if off not in cols:
                cols[off] = column(off[0] * nc + off[1], off[0])
            tiles[n] = ub[rd, n] + couplings[n] * cols[off]
        return tiles, gamma, curve

    for n, copy in enumerate(load_copies):
        copy.wait_recv()
    own_lookup = (own_position, own_active)
    load_tiles = {n: (loads[...] if n == 0 else loads_n[n]) for n in range(len(near))}
    start = jump_at(load_tiles, 0, 0, own_lookup)
    count = publish(0, start, None, True)

    for copy in part_copies:
        copy.wait_recv()
    for copy in cpl_copies:
        copy.wait_recv()
    lookups = [own_lookup] + [index_of(part_n[n]) for n in range(1, len(near))]
    couplings = [coupling] + [spread(cpl_n[n]) for n in range(1, len(slots))]
    bytes_k = kc.at[pl.ds(1, ndev - 1)]
    pltpu.make_async_copy(bytes_k, bytes_k, k_recv).wait()

    def widen(k, di, dj):
        kt[k] = jnp.where(of_rhs, spread(kc[k]), 0.0)

    others(widen)
    fetches[5].wait()
    for copy in d_copies:
        copy.wait_recv()
    east, west = near.index(east_off), near.index(west_off)
    upright = [n for n in range(len(near)) if n not in (east, west)]

    def edge_into(n, s, pair, at):
        first = facing_start[near[n]]
        high, low = split(dnear[n, s].T)
        pair[at * width : (at + 1) * width, first : first + edge] = high
        pair[at * width : (at + 1) * width, width + first : width + first + edge] = low

    split_into(dpair.at[0], [dbuf[s] for s in range(sc)])
    for n in upright[1:]:
        for s in range(sc):
            edge_into(n, s, dpair.at[n], s)
    edge_into(east, 0, dpair.at[east], 0)
    edge_into(west, sc - 1, dpair.at[east], 1)
    tiles, _, _ = collect(0, count, False)
    residual = [jump_at(tiles, *near[n], lookups[n]) for n in range(len(near))]

    multipliers = jnp.zeros((rows, width), jnp.float32)
    search = along = gamma = step_size = None
    for iteration in range(ITERS):
        rd = iteration + 1
        last = rd == ITERS
        weighted = {}
        for n in upright:
            weighted[n] = multiply(2.0 * residual[n], dpair[n], sc)
        beside = jnp.where(row < nrhs, residual[east], residual[west])
        weighted[east] = weighted[west] = multiply(2.0 * beside, dpair[east, pl.ds(0, 2 * width)], 2)
        precon = jump_at(weighted, 0, 0, own_lookup)
        doubled = 2.0 * precon
        count = publish(rd, doubled, (residual[0] * precon, doubled), not last)
        tiles, gamma_new, curve = collect(rd, count, True)
        kept = 1 if last else len(near)
        image = [jump_at(tiles, *near[n], lookups[n]) for n in range(kept)]
        if iteration == 0:
            step_size = gamma_new / curve
            search, along = precon, image
        else:
            ratio = gamma_new / gamma
            step_size = gamma_new / (curve - ratio * gamma_new / step_size)
            search = precon + ratio * search
            along = [image[n] + ratio * along[n] for n in range(kept)]
        gamma = gamma_new
        multipliers = multipliers + step_size * search
        residual = [residual[n] - step_size * along[n] for n in range(kept)]
    out[0] = multipliers
    out[1] = residual[0]

    for copy in load_copies + part_copies + cpl_copies + d_copies:
        copy.wait_send()
    pltpu.make_async_copy(bytes_k, bytes_k, k_send).wait()
    for rd in range(ITERS + 1):
        bytes_q = qb.at[rd, pl.ds(1, ndev - 1)]
        pltpu.make_async_copy(bytes_q, bytes_q, q_send.at[rd]).wait()
        sent = (len(near) if rd == ITERS else len(slots)) - 1
        bytes_u = ub.at[rd, pl.ds(1, sent)]
        pltpu.make_async_copy(bytes_u, bytes_u, u_send.at[rd]).wait()


def solution(mesh):
    nr, nc = mesh.shape["srow"], mesh.shape["scol"]
    near, slots = slot_list(nr, nc)

    def body(loads, local_inverse, dirichlet, corner_coupling, coarse_inverse, partner):
        sr, sc, nrhs, width = loads.shape
        rows = sr * sc * nrhs
        ndev = nr * nc
        lanes = -(-(nrhs * nc * sc + 2 * nrhs) // 128) * 128
        dma = pltpu.SemaphoreType.DMA
        f32 = jnp.float32
        vmem = pl.BlockSpec(memory_space=pltpu.VMEM)
        hbm = pl.BlockSpec(memory_space=pl.ANY)
        rounds = ITERS + 1
        out = pl.pallas_call(
            functools.partial(kernel, nr, nc, near, slots, sc, nrhs),
            out_shape=pltpu.VMEM((2, rows, width), f32),
            in_specs=[hbm] * 6,
            out_specs=vmem,
            scratch_shapes=[
                pltpu.VMEM((rows, width), f32),
                pltpu.VMEM((sc, width), f32),
                pltpu.VMEM((sc, coarse_inverse.shape[-1]), f32),
                pltpu.VMEM((sc, width), jnp.int32),
                pltpu.VMEM((sc, width, width), f32),
                pltpu.VMEM((sc, width, width), f32),
                pltpu.VMEM((sc * width, 2 * width), jnp.bfloat16),
                pltpu.VMEM((len(near), sc * width, 2 * width), jnp.bfloat16),
                pltpu.VMEM((len(near), rows, width), f32),
                pltpu.VMEM((len(near), sc, width), jnp.int32),
                pltpu.VMEM((len(slots), sc, width), f32),
                pltpu.VMEM((len(near), sc, width // 4, width), f32),
                pltpu.VMEM((ndev, sc, lanes), f32),
                pltpu.VMEM((ndev, rows, lanes), f32),
                pltpu.VMEM((rounds, len(slots), rows, width), f32),
                pltpu.VMEM((rounds, ndev, 1, lanes), f32),
                dma((6,)), dma, dma,
                dma((len(slots),)), dma((len(slots),)),
                dma((len(near),)), dma((len(near),)),
                dma((len(near),)), dma((len(near),)),
                dma((len(near),)), dma((len(near),)),
                dma((rounds,)), dma((rounds,)),
                dma((rounds,)), dma((rounds,)),
            ],
            compiler_params=pltpu.CompilerParams(collective_id=0, has_side_effects=True),
        )(
            loads.reshape(rows, width),
            corner_coupling.reshape(sc, width),
            coarse_inverse.reshape(sc, coarse_inverse.shape[-1]),
            partner.reshape(sc, width),
            local_inverse.reshape(sc, width, width),
            dirichlet.reshape(sc, width, width),
        )
        return out[0].reshape(loads.shape), out[1].reshape(loads.shape)

    return jax.shard_map(
        body,
        mesh=mesh,
        in_specs=(
            P("srow", "scol", None, None),
            P("srow", "scol", None, None),
            P("srow", "scol", None, None),
            P("srow", "scol", None),
            P("srow", "scol", None),
            P("srow", "scol", None),
        ),
        out_specs=(P("srow", "scol", None, None), P("srow", "scol", None, None)),
        check_vma=False,
    )
```

profile of v0, /device:TPU:0, one launch (start us, length us, event | category | flops | bytes accessed | tf_op | source)
XLA Modules:
  0.0 31.6 jit_solution(10376943092767058145)
XLA Ops:
  0.6 30.3 %shard_map.77 = f32[2,8,128]{2,1,0:T(8,128)S(1)} custom-call(f32[8,128]{1,0:T(8,128)} %bitcast.10, f32[2,128]{1,0:T(2,128)} %bitcast.13, f32[2,16]{1,0:T(2,128)} %bitcast.14, s32[2,128]{1,0:T(2,128)} %bitcast.15, f32[2,128,128]{2,1,0:T(8,128)} %bitcast.8, f32[2,128,128]{2,1,0:T(8,128)} %bitcast.9), custom_call_target="tpu_custom_call" | custom-call | tf_op jit(solution)/shard_map/pallas_call | solution.py:334
  31.0 0.6 %fusion = (f32[1,8,128]{2,1,0:T(8,128)}, f32[1,8,128]{2,1,0:T(8,128)}) fusion(f32[2,8,128]{2,1,0:T(8,128)S(1)} %shard_map.77), kind=kLoop, calls=%fused_computation | loop fusion | bytes 16384 | tf_op jit(solution)/shard_map/slice | solution.py:373
where the time goes:
time: 31.7 us; the launch traced here: 31.6 us
  Pallas kernels  30.3 us (96%)
  between operations  0.64 us (2%)
  local copies, waits for them, and re-layouts  0.6 us (2%)
    pallas_call x1, Pallas kernels, body(): pl.pallas_call(functools.partial(kernel, nr, nc, near, slots, sc, nrhs),...  30.3 us

commit v1 on v0

--- a/solution.py
+++ b/solution.py
@@ -168,19 +168,19 @@
         return jump(tiles[slot_of(di, dj)], tile(di, dj - 1), tile(di, dj + 1), tile(di - 1, dj), tile(di + 1, dj), lookup)
 
     def multiply(values, pair, count):
+        total = values.shape[0]
         high, low = split(values)
         stacked = jnp.concatenate([high.astype(jnp.float32), low.astype(jnp.float32)], axis=0)
         sub = lax.rem(lax.div(lax.broadcasted_iota(jnp.int32, stacked.shape, 0), nrhs), sc)
         wide = jnp.concatenate(
             [jnp.where(sub == (s if s < count - 1 else sc - 1), stacked, 0.0) for s in range(count)], axis=1)
         product = jnp.dot(wide.astype(jnp.bfloat16), pair, preferred_element_type=jnp.float32)
-        return (product[0:rows, 0:width] + product[rows:, 0:width]) + (product[0:rows, width:] + product[rows:, width:])
+        return (product[0:total, 0:width] + product[total:, 0:width]) + (product[0:total, width:] + product[total:, width:])
 
     def lane_sum(values):
         return jnp.sum(values, axis=1, keepdims=True)
 
-    def publish(rd, values, dots, wide):
-        u = multiply(values, lpair[...], sc)
+    def publish(rd, values, u, dots, wide):
         ub[rd, 0] = u
         count = len(slots) if wide else len(near)
         for n in range(1, count):
@@ -198,7 +198,12 @@
         others(send_q)
         return count
 
-    def collect(rd, count, want_dots):
+    def collect_tiles(rd, count):
+        bytes_u = ub.at[rd, pl.ds(1, count - 1)]
+        pltpu.make_async_copy(bytes_u, bytes_u, u_recv.at[rd]).wait()
+        return {n: ub[rd, n] for n in range(count)}
+
+    def collect_sums(rd, count, want_dots):
         bytes_q = qb.at[rd, pl.ds(1, ndev - 1)]
         pltpu.make_async_copy(bytes_q, bytes_q, q_recv.at[rd]).wait()
         band = [jnp.broadcast_to(jnp.sum(qb[rd, pl.ds(d * nc, nc)], axis=0), (rows, lanes)) for d in range(nr)]
@@ -225,22 +230,46 @@
             crossed = jnp.broadcast_to(jnp.sum(cross, axis=0, keepdims=True), (rows, lanes))
             curve = lane_sum(jnp.where(of_rhs, crossed, 0.0) + jnp.where(curve_lane, everything, 0.0))
             gamma = lane_sum(jnp.where(gamma_lane, everything, 0.0))
-        bytes_u = ub.at[rd, pl.ds(1, count - 1)]
-        pltpu.make_async_copy(bytes_u, bytes_u, u_recv.at[rd]).wait()
-        tiles = {}
         for n in range(count):
             off = slots[n]
             if off not in cols:
                 cols[off] = column(off[0] * nc + off[1], off[0])
-            tiles[n] = ub[rd, n] + couplings[n] * cols[off]
-        return tiles, gamma, curve
+        turned = {}
+        for n in range(count):
+            wide_col = jnp.broadcast_to(cols[slots[n]], (rows, width))
+            for m in range(sc):
+                turned[n, m] = pltpu.roll(wide_col, m * nrhs, 0) if m else wide_col
+        return turned, gamma, curve
+
+    def precondition(images):
+        weighted = {}
+        for n in upright:
+            weighted[n] = multiply(2.0 * images[n], dpair[n], sc)
+        high = lax.rem(lax.broadcasted_iota(jnp.int32, images[east].shape, 0), rows) < nrhs
+        beside = jnp.where(high, images[east], images[west])
+        weighted[east] = weighted[west] = multiply(2.0 * beside, dpair[east, pl.ds(0, 2 * width)], 2)
+        return weighted
+
+    def advance(tiles, keep):
+        images = [jump_at(tiles, *near[n], lookups[n]) for n in range(len(near) if keep else 1)]
+        if not keep:
+            return images[0], None, None
+        weighted = precondition(images)
+        step = jump_at(weighted, 0, 0, own_lookup)
+        return images[0], step, multiply(2.0 * step, lpair[...], sc)
+
+    def coarse(base, table, turned, count):
+        for n in range(count):
+            for m in range(sc):
+                base = base + table[n, m] * turned[n, m]
+        return base
 
     for n, copy in enumerate(load_copies):
         copy.wait_recv()
     own_lookup = (own_position, own_active)
     load_tiles = {n: (loads[...] if n == 0 else loads_n[n]) for n in range(len(near))}
     start = jump_at(load_tiles, 0, 0, own_lookup)
-    count = publish(0, start, None, True)
+    count = publish(0, start, multiply(start, lpair[...], sc), None, True)
 
     for copy in part_copies:
         copy.wait_recv()
@@ -273,38 +302,81 @@
             edge_into(n, s, dpair.at[n], s)
     edge_into(east, 0, dpair.at[east], 0)
     edge_into(west, sc - 1, dpair.at[east], 1)
-    tiles, _, _ = collect(0, count, False)
-    residual = [jump_at(tiles, *near[n], lookups[n]) for n in range(len(near))]
+    group = nrhs // sc
+    wrhs_row = lax.rem(row, nrhs)
+    wsub_row = lax.div(row, nrhs)
+    nothing = jnp.zeros((rows, width), jnp.float32)
+    batches = [list(range(first, min(first + group, len(slots)))) for first in range(0, len(slots), group)]
+    basis_images = []
+    for batch in batches:
+        tiles = {n: nothing for n in range(len(slots))}
+        for g, n in enumerate(batch):
+            tiles[n] = jnp.where(wrhs_row == g * sc + wsub_row, couplings[n], 0.0)
+        basis_images.append([jump_at(tiles, *near[n], lookups[n]) for n in range(len(near))])
+    stacked = [jnp.concatenate([images[n] for images in basis_images], axis=0) for n in range(len(near))]
+    basis_weighted = precondition(stacked)
+    basis_steps = []
+    for b in range(len(batches)):
+        part_of = {n: basis_weighted[n][b * rows : (b + 1) * rows] for n in range(len(near))}
+        basis_steps.append(jump_at(part_of, 0, 0, own_lookup))
+    stacked_step = jnp.concatenate(basis_steps, axis=0)
+    stacked_u = multiply(2.0 * stacked_step, lpair[...], sc)
+
+    def table_of(stack, count):
+        table = {}
+        for n in range(count):
+            first = (n // group) * rows + (n % group) * sc
+            for m in range(sc):
+                value = None
+                for s in range(sc):
+                    at = first + s * nrhs + (s - m) % sc
+                    line = jnp.broadcast_to(stack[at : at + 1], (rows, width))
+                    value = line if value is None else jnp.where(wsub_row == s, line, value)
+                table[n, m] = value
+        return table
+
+    image_table = table_of(stacked[0], len(near))
+    step_table = table_of(stacked_step, len(slots))
+    u_table = table_of(stacked_u, len(slots))
+
+    image, step, lifted = advance(collect_tiles(0, count), True)
+    turned, _, _ = collect_sums(0, count, False)
+    residual = coarse(image, image_table, turned, len(near))
+    precon = coarse(step, step_table, turned, len(slots))
+    u = coarse(lifted, u_table, turned, len(slots))
 
     multipliers = jnp.zeros((rows, width), jnp.float32)
-    search = along = gamma = step_size = None
+    search = along = steps = lifts = gamma = step_size = None
     for iteration in range(ITERS):
         rd = iteration + 1
         last = rd == ITERS
-        weighted = {}
-        for n in upright:
-            weighted[n] = multiply(2.0 * residual[n], dpair[n], sc)
-        beside = jnp.where(row < nrhs, residual[east], residual[west])
-        weighted[east] = weighted[west] = multiply(2.0 * beside, dpair[east, pl.ds(0, 2 * width)], 2)
-        precon = jump_at(weighted, 0, 0, own_lookup)
         doubled = 2.0 * precon
-        count = publish(rd, doubled, (residual[0] * precon, doubled), not last)
-        tiles, gamma_new, curve = collect(rd, count, True)
-        kept = 1 if last else len(near)
-        image = [jump_at(tiles, *near[n], lookups[n]) for n in range(kept)]
+        count = publish(rd, doubled, u, (residual * precon, doubled), not last)
+        image, step, lifted = advance(collect_tiles(rd, count), not last)
+        turned, gamma_new, curve = collect_sums(rd, count, True)
+        image = coarse(image, image_table, turned, len(near))
+        if not last:
+            step = coarse(step, step_table, turned, len(slots))
+            lifted = coarse(lifted, u_table, turned, len(slots))
         if iteration == 0:
             step_size = gamma_new / curve
-            search, along = precon, image
+            search, along, steps, lifts = precon, image, step, lifted
         else:
             ratio = gamma_new / gamma
             step_size = gamma_new / (curve - ratio * gamma_new / step_size)
             search = precon + ratio * search
-            along = [image[n] + ratio * along[n] for n in range(kept)]
+            along = image + ratio * along
+            if not last:
+                steps = step + ratio * steps
+                lifts = lifted + ratio * lifts
         gamma = gamma_new
         multipliers = multipliers + step_size * search
-        residual = [residual[n] - step_size * along[n] for n in range(kept)]
+        residual = residual - step_size * along
+        if not last:
+            precon = precon - step_size * steps
+            u = u - step_size * lifts
     out[0] = multipliers
-    out[1] = residual[0]
+    out[1] = residual
 
     for copy in load_copies + part_copies + cpl_copies + d_copies:
         copy.wait_send()

time: 31.7 us -> 30.5 us (0.962)
  Pallas kernels: 30.3 us -> 29.1 us
    pallas_call x1, Pallas kernels: 30.3 us -> 29.1 us  [body(): pl.pallas_call(functools.partial(kernel, nr, nc, near, slots, sc, nrhs),...]
where the time goes in v1:
time: 30.5 us; the launch traced here: 30.3 us
  Pallas kernels  29.1 us (95%)
  between operations  0.64 us (2%)
  local copies, waits for them, and re-layouts  0.6 us (2%)
    pallas_call x1, Pallas kernels, body(): pl.pallas_call(functools.partial(kernel, nr, nc, near, slots, sc, nrhs),...  29.1 us

profile of v1, /device:TPU:0, one launch (start us, length us, event | category | flops | bytes accessed | tf_op | source)
XLA Modules:
  0.0 30.3 jit_solution(5709798077001446779)
XLA Ops:
  0.6 29.1 %shard_map.77 = f32[2,8,128]{2,1,0:T(8,128)S(1)} custom-call(f32[8,128]{1,0:T(8,128)} %bitcast.10, f32[2,128]{1,0:T(2,128)} %bitcast.13, f32[2,16]{1,0:T(2,128)} %bitcast.14, s32[2,128]{1,0:T(2,128)} %bitcast.15, f32[2,128,128]{2,1,0:T(8,128)} %bitcast.8, f32[2,128,128]{2,1,0:T(8,128)} %bitcast.9), custom_call_target="tpu_custom_call" | custom-call | tf_op jit(solution)/shard_map/pallas_call | solution.py:406
  29.7 0.6 %fusion = (f32[1,8,128]{2,1,0:T(8,128)}, f32[1,8,128]{2,1,0:T(8,128)}) fusion(f32[2,8,128]{2,1,0:T(8,128)S(1)} %shard_map.77), kind=kLoop, calls=%fused_computation | loop fusion | bytes 16384 | tf_op jit(solution)/shard_map/slice | solution.py:445

commit v2 on v0

v2 whole, which is shorter than its diff:
```python
import functools

import jax
import jax.numpy as jnp
from jax import lax
from jax.experimental import pallas as pl
from jax.experimental.pallas import tpu as pltpu
from jax.sharding import PartitionSpec as P

ITERS = 3
MESH = pl.DeviceIdType.MESH
precise = lax.Precision.HIGHEST
UNROLL = 64
EAST, WEST, SOUTH, NORTH = 2, 4, 6, 7


def block_slots(nb, nc):
    slots = []
    for dp, dj in ((0, 0), (0, 1), (0, -1), (1, 1), (1, -1), (-1, 1), (-1, -1), (1, 0), (-1, 0)):
        off = (dp % nb, dj % nc)
        if off not in slots:
            slots.append(off)
    return slots


def kernel(nr, nc, slots, sc, nrhs, loads_in, cpl_in, cinv_in, part_in, linv, dirich, out,
           cinv, loads, cpl, part, lbuf, dbuf, lpair, dpair, fpair, loads_n, part_n, cpl_n, dside, dflat, kc, kt, ub, qb,
           local_sem, send_sem, recv_sem, u_send, u_recv, q_send, q_recv):
    rows, width = loads_n.shape[1:]
    edge = width // 4
    ndev = nr * nc
    nb = nr // 2
    nblocks = nb * nc
    ncols = nc * sc
    lanes = kt.shape[-1]
    i, j = lax.axis_index("srow"), lax.axis_index("scol")
    p, core = lax.div(i, 2), lax.rem(i, 2)
    near = [(0, 0), (1, 0), (0, 1), (1, 1), (0, nc - 1), (1, nc - 1), (nr - 1, 0), (2, 0)]
    LOADS, PART, CPL, LINV, DIRICH, SIDE, FLAT, KROW = range(8)

    def others(step):
        if ndev <= UNROLL:
            far_first = sorted(range(1, ndev), key=lambda k: (-min(k // nc, nr - k // nc), min(k % nc, nc - k % nc) % (nc // 2)))
            for k in far_first:
                step(lax.rem(i + k // nc, nr), lax.rem(j + k % nc, nc))
        else:
            @pl.loop(1, ndev)
            def _(k):
                step(lax.rem(i + lax.div(k, nc), nr), lax.rem(j + lax.rem(k, nc), nc))

    barrier = pltpu.get_barrier_semaphore()

    def greet(ti, tj):
        pl.semaphore_signal(barrier, inc=1, device_id=(ti, tj), device_id_type=MESH)

    others(greet)

    fetches = [
        pltpu.make_async_copy(src, dst, local_sem.at[n])
        for n, (src, dst) in enumerate((
            (cinv_in, cinv), (loads_in, loads), (cpl_in, cpl), (part_in, part),
            (linv, lbuf.at[core]), (dirich, dbuf.at[core]),
        ))
    ]
    for fetch in fetches:
        fetch.start()

    row = lax.broadcasted_iota(jnp.int32, (rows, width), 0)
    lane = lax.broadcasted_iota(jnp.int32, (rows, width), 1)
    wrow = lax.broadcasted_iota(jnp.int32, (rows, lanes), 0)
    wlane = lax.broadcasted_iota(jnp.int32, (rows, lanes), 1)
    wrhs = lax.rem(wrow, nrhs)
    wsub = lax.div(wrow, nrhs)
    of_rhs = lax.div(wlane, ncols) == wrhs
    gamma_lane = wlane == nrhs * ncols + wrhs
    curve_lane = wlane == nrhs * ncols + nrhs + wrhs
    rhs_row = lax.rem(row, nrhs)
    sub_row = lax.div(row, nrhs)

    def spread(block):
        out = jnp.broadcast_to(block[0:1], (rows, block.shape[1]))
        which = lax.div(lax.broadcasted_iota(jnp.int32, out.shape, 0), nrhs)
        for s in range(1, sc):
            out = jnp.where(which == s, jnp.broadcast_to(block[s : s + 1], out.shape), out)
        return out

    def place(dj):
        column = lax.rem(j + dj, nc) * sc
        return wlane == wrhs * ncols + column + wsub

    def pick(values, index):
        return jnp.take_along_axis(values, index, axis=1, mode="promise_in_bounds")

    side = lax.div(lane, edge)
    half = lax.rem(side, 2)

    def odd(dr):
        return lax.rem(sub_row + dr, 2)

    def split(values):
        high = values.astype(jnp.bfloat16)
        return high, (values - high.astype(jnp.float32)).astype(jnp.bfloat16)

    def split_into(pair, blocks):
        for s, block in enumerate(blocks):
            high, low = split(block)
            pair[s * width : (s + 1) * width, 0:width] = high
            pair[s * width : (s + 1) * width, width : 2 * width] = low

    tile_lane = lax.broadcasted_iota(jnp.int32, (ncols, lanes), 1)
    tile_row = lax.broadcasted_iota(jnp.int32, (ncols, lanes), 0)
    tiler = jnp.where(lax.rem(tile_lane, ncols) == tile_row, 1.0, 0.0)
    for fetch in fetches[:4]:
        fetch.wait()
    tiled = jnp.dot(spread(cinv[...]), tiler, precision=precise, preferred_element_type=jnp.float32)
    for s in range(sc):
        kc[core * nc, s : s + 1] = tiled[s * nrhs : s * nrhs + 1]
    own_place = place(0)
    partner = spread(part[...])
    other = edge * (1 - 2 * half)
    mirrored = jnp.where((half == 1) & (partner >= 0), partner + side * edge, lane)
    crossed_over = jnp.where(half == 0, pltpu.roll(mirrored, width - edge, 1), pltpu.roll(mirrored, edge, 1))
    own_odd = odd(core)
    forward = jnp.where(own_odd == 1, crossed_over, mirrored)
    backward = jnp.where(own_odd == 1, mirrored + other, mirrored)
    loads_n[core] = pick(loads[...], forward)
    active_own = pick(jnp.where(partner >= 0, 1.0, 0.0), forward)
    coupling_own = pick(spread(cpl[...]), forward)
    for s in range(sc):
        part_n[core, s : s + 1] = active_own[s * nrhs : s * nrhs + 1]
        cpl_n[core, s : s + 1] = coupling_own[s * nrhs : s * nrhs + 1]

    def reorder(buffer):
        for s in range(sc):
            index = jnp.broadcast_to(forward[s * nrhs : s * nrhs + 1], (width, width))
            buffer[core, s] = pick(pick(buffer[core, s], index).T, index)

    pl.semaphore_wait(barrier, ndev - 1)

    def push(src, dst, what, ti, tj):
        pltpu.make_async_remote_copy(
            src_ref=src, dst_ref=dst, send_sem=send_sem.at[what], recv_sem=recv_sem.at[what],
            device_id=(ti, tj), device_id_type=MESH).start()

    west_j, east_j = lax.rem(j + nc - 1, nc), lax.rem(j + 1, nc)
    beyond = lax.rem(p + 2 * core - 1 + nb, nb)
    partner_i = i + 1 - 2 * core
    around = [(EAST + core, 2 * p + t, west_j) for t in range(2)] + [(WEST + core, 2 * p + t, east_j) for t in range(2)]
    around += [(NORTH - core, 2 * beyond + t, j) for t in range(2)]
    toward = around + [(core, partner_i, j)]
    for n, ti, tj in toward:
        push(loads_n.at[core], loads_n.at[n], LOADS, ti, tj)
    for n, ti, tj in toward:
        push(part_n.at[core], part_n.at[n], PART, ti, tj)
    for n, (dp, dj) in enumerate(slots):
        for t in range(2):
            ti, tj = 2 * lax.rem(p - dp + nb, nb) + t, lax.rem(j - dj + nc, nc)
            if (dp, dj) == (0, 0):
                if t == 0:
                    push(cpl_n.at[core], cpl_n.at[core], CPL, partner_i, j)
            else:
                push(cpl_n.at[core], cpl_n.at[2 * n + core], CPL, ti, tj)
    def send_k(ti, tj):
        slot = lax.rem(i - 2 * lax.div(ti, 2) + nr, nr) * nc + lax.rem(j - tj + nc, nc)
        push(kc.at[core * nc], kc.at[slot], KROW, ti, tj)

    others(send_k)
    fetches[4].wait()
    reorder(lbuf)
    push(lbuf.at[core], lbuf.at[core], LINV, partner_i, j)
    fetches[5].wait()
    reorder(dbuf)

    def facing_rows(s, group):
        return dbuf.at[core, s, pl.ds(pl.multiple_of(group * edge, edge), edge)]

    for n, ti, tj in around[:2]:
        push(facing_rows(0, lax.rem(core, 2)), dside.at[core], SIDE, ti, tj)
    for n, ti, tj in around[2:4]:
        push(facing_rows(sc - 1, 1 - lax.rem(core + sc - 1, 2)), dside.at[2 + core], SIDE, ti, tj)
    for n, ti, tj in around[4:]:
        for s in range(sc):
            push(facing_rows(s, 2 + s % 2), dflat.at[1 - core, s], FLAT, ti, tj)
    push(dbuf.at[core], dbuf.at[core], DIRICH, partner_i, j)

    arrivals = {
        LOADS: loads_n.at[pl.ds(0, 7)], PART: part_n.at[pl.ds(0, 7)], CPL: cpl_n.at[pl.ds(0, 2 * len(slots) - 1)],
        LINV: lbuf.at[0], DIRICH: dbuf.at[0], SIDE: dside, FLAT: dflat, KROW: kc.at[pl.ds(0, ndev - 1)],
    }

    def arrived(what):
        pltpu.make_async_copy(arrivals[what], arrivals[what], recv_sem.at[what]).wait()

    def left(what):
        pltpu.make_async_copy(arrivals[what], arrivals[what], send_sem.at[what]).wait()

    def meet(mine, before, after, south, north, dr, active):
        if rows == 2 * nrhs:
            lateral = pltpu.roll(jnp.where(half == odd(dr + 1), before, after), nrhs, 0)
        else:
            lateral = jnp.where(half == odd(dr), pltpu.roll(before, nrhs, 0), pltpu.roll(after, rows - nrhs, 0))
        facing = jnp.where(side < 2, lateral, jnp.where(half == odd(dr), south, north))
        return jnp.where(active, mine - facing, 0.0)

    def jump(mine, west_tile, east_tile, south, north, dr, active):
        before = jnp.where(row < rows - nrhs, mine, west_tile)
        after = jnp.where(row < nrhs, east_tile, mine)
        return meet(mine, before, after, south, north, dr, active)

    def key(dr, dj):
        return (dr % nr, dj % nc)

    def jump_at(tiles, dr, dj, lookup):
        mine = tiles[key(dr, dj)]
        beyond = [tiles.get(key(*at), mine) for at in ((dr, dj - 1), (dr, dj + 1), (dr - 1, dj), (dr + 1, dj))]
        return jump(mine, *beyond, dr, lookup)

    def multiply(values, pair):
        total = values.shape[0]
        high, low = split(values)
        stacked = jnp.concatenate([high.astype(jnp.float32), low.astype(jnp.float32)], axis=0)
        sub = lax.rem(lax.div(lax.broadcasted_iota(jnp.int32, stacked.shape, 0), nrhs), sc)
        wide = jnp.concatenate([jnp.where(sub == s, stacked, 0.0) for s in range(sc)], axis=1)
        product = jnp.dot(wide.astype(jnp.bfloat16), pair, preferred_element_type=jnp.float32)
        return (product[0:total, 0:width] + product[total:, 0:width]) + (product[0:total, width:] + product[total:, width:])

    def lane_sum(values):
        return jnp.sum(values, axis=1, keepdims=True)

    keys = {key(2 * dp + a, dj): (n, a) for n, (dp, dj) in enumerate(slots) for a in range(2)}

    def reach(a, at):
        return min((at[0] - a) % nr, (a - at[0]) % nr) + min(at[1], nc - at[1])

    def flip(index, mask):
        for bit in range(mask.bit_length()):
            if mask >> bit & 1:
                index = index + (1 << bit) - (2 << bit) * lax.rem(lax.div(index, 1 << bit), 2)
        return index

    powers = nb & (nb - 1) == 0 and nc & (nc - 1) == 0
    masks = sorted(((a, b) for a in range(nb) for b in range(nc) if a or b), key=lambda m: -(m[0] + m[1] // 2 + m[1] % 2))

    def q_target(tp, tj):
        return lax.rem(p - tp + nb, nb) * nc + lax.rem(j - tj + nc, nc), 2 * tp + 1 - core, tj

    q_targets = []
    if nblocks <= UNROLL:
        for a, b in masks:
            q_targets.append(q_target(flip(p, a), flip(j, b)) if powers else q_target(lax.rem(p + a, nb), lax.rem(j + b, nc)))
    u_targets = [
        (n, 2 * lax.rem(p - dp + nb, nb) + 1 - core, lax.rem(j - dj + nc, nc)) for n, (dp, dj) in enumerate(slots) if n
    ]
    u_targets.sort(key=lambda target: (slots[target[0]][1] == 0, slots[target[0]][0] == 0))

    def publish(rd, values, u, dots):
        for a in range(2):
            ub[rd, 0, a] = u[a]

        def across(src, dst, send, recv, ti, tj):
            pltpu.make_async_remote_copy(
                src_ref=src, dst_ref=dst, send_sem=send.at[rd], recv_sem=recv.at[rd],
                device_id=(ti, tj), device_id_type=MESH).start()

        for n, ti, tj in u_targets:
            across(ub.at[rd, 0], ub.at[rd, n], u_send, u_recv, ti, tj)
        for a in range(2):
            message = jnp.where(own_place, lane_sum(couplings[a, 0] * values[a]), 0.0)
            if dots is not None and a == 0:
                gamma, curve = dots
                message = jnp.where(gamma_lane, lane_sum(gamma), message)
                message = jnp.where(curve_lane, lane_sum(curve), message)
            qb[rd, 0, a : a + 1] = jnp.sum(message, axis=0, keepdims=True)
        if nblocks <= UNROLL:
            for slot, ti, tj in q_targets:
                across(qb.at[rd, 0], qb.at[rd, slot], q_send, q_recv, ti, tj)
        else:
            @pl.loop(1, nblocks)
            def _(k):
                slot, ti, tj = q_target(lax.rem(p + lax.div(k, nc), nb), lax.rem(j + lax.rem(k, nc), nc))
                across(qb.at[rd, 0], qb.at[rd, slot], q_send, q_recv, ti, tj)

    def sent(rd):
        bytes_q = qb.at[rd, pl.ds(1, nblocks - 1)]
        pltpu.make_async_copy(bytes_q, bytes_q, q_send.at[rd]).wait()
        bytes_u = ub.at[rd, pl.ds(1, len(slots) - 1)]
        pltpu.make_async_copy(bytes_u, bytes_u, u_send.at[rd]).wait()

    def collect_tiles(rd):
        bytes_u = ub.at[rd, pl.ds(1, len(slots) - 1)]
        pltpu.make_async_copy(bytes_u, bytes_u, u_recv.at[rd]).wait()
        bytes_q = qb.at[rd, pl.ds(1, nblocks - 1)]
        pltpu.make_async_copy(bytes_q, bytes_q, q_recv.at[rd]).wait()
        return {at: ub[rd, n, a] for at, (n, a) in keys.items()}

    def collect_sums(rd, want_dots):
        sums = [jnp.sum(qb[rd, pl.ds(d * nc, nc)], axis=0) for d in range(nb)]
        band = [jnp.broadcast_to(sums[d // 2][d % 2 : d % 2 + 1], (rows, lanes)) for d in range(nr)]
        cols = {}

        def column(k, d):
            return lane_sum(band[d] * kt[k])

        gamma = curve = None
        if want_dots:
            cross = jnp.zeros((rows, lanes), jnp.float32)
            for d in range(nr):
                total = jnp.zeros((rows, lanes), jnp.float32)
                if ndev <= UNROLL:
                    for e in range(nc):
                        cols[(d, e)] = column(d * nc + e, d)
                        total = total + jnp.where(place(e), cols[(d, e)], 0.0)
                else:
                    def add(e, total):
                        return total + jnp.where(place(e), column(d * nc + e, d), 0.0)
                    total = lax.fori_loop(0, nc, add, total)
                cross = cross + total * band[d]
            everything = functools.reduce(jnp.add, band)
            crossed = jnp.broadcast_to(jnp.sum(cross, axis=0, keepdims=True), (rows, lanes))
            curve = lane_sum(jnp.where(of_rhs, crossed, 0.0) + jnp.where(curve_lane, everything, 0.0))
            gamma = lane_sum(jnp.where(gamma_lane, everything, 0.0))
        turned = {}
        for at in keys:
            if at not in cols:
                cols[at] = column(at[0] * nc + at[1], at[0])
            wide_col = jnp.broadcast_to(cols[at], (rows, width))
            for m in range(sc):
                turned[at, m] = pltpu.roll(wide_col, m * nrhs, 0) if m else wide_col
        return turned, gamma, curve

    def beside(a):
        return [key(a, 1), key(2, 0) if a else key(-1, 0)]

    def precondition(images):
        weighted = []
        for a in range(2):
            total = images[key(a, 0)].shape[0]
            ring = multiply(2.0 * jnp.concatenate([images[at] for at in beside(a)], axis=0), fpair[a])
            weighted.append({at: ring[m * total : (m + 1) * total] for m, at in enumerate(beside(a))})
            weighted[a][key(a, -1)] = weighted[a][key(a, 1)]
        for a in range(2):
            mine = multiply(2.0 * images[key(a, 0)], dpair[a])
            for ring in weighted:
                ring[key(a, 0)] = mine
        return weighted

    def jump_sides(tiles, a):
        east, mine, west = (tiles[key(a, dj)] for dj in (1, 0, -1))
        before = jnp.where(row < rows - nrhs, west, mine)
        after = jnp.where(row < nrhs, mine, east)
        flat = [jnp.where(row < nrhs, tiles.get(key(a + d, 1), east), tiles.get(key(a + d, -1), west)) for d in (-1, 1)]
        return meet(jnp.where(row < nrhs, east, west), before, after, *flat, a, side_lookups[a])

    def images_of(tiles):
        images = {key(*near[n]): jump_at(tiles, *near[n], lookups[n]) for n in (0, 1, SOUTH, NORTH)}
        for a in range(2):
            images[key(a, 1)] = jump_sides(tiles, a)
        return images

    def advance(tiles, keep):
        if not keep:
            return [jump_at(tiles, a, 0, lookups[a]) for a in range(2)], None, None
        images = images_of(tiles)
        weighted = precondition(images)
        step = [jump_at(weighted[a], a, 0, lookups[a]) for a in range(2)]
        return [images[key(a, 0)] for a in range(2)], step, [multiply(2.0 * step[a], lpair[a]) for a in range(2)]

    def coarse(base, table, turned):
        out = []
        for a in range(2):
            value = base[a]
            for at, m in table[a]:
                value = value + table[a][at, m] * turned[at, m]
            out.append(value)
        return out

    arrived(LINV)
    for a in range(2):
        split_into(lpair.at[a], [lbuf[a, s] for s in range(sc)])
        fpair[a] = jnp.zeros(fpair.shape[1:], jnp.bfloat16)

    arrived(PART)
    partners = [spread(part_n[n]) for n in range(len(near))]
    lookups = [partner > 0.5 for partner in partners]
    side_lookups = [jnp.where(row < nrhs, partners[EAST + a], partners[WEST + a]) > 0.5 for a in range(2)]
    arrived(CPL)
    couplings = {at: spread(cpl_n[2 * n + a]) for at, (n, a) in keys.items()}
    arrived(LOADS)
    load_tiles = {key(*at): loads_n[n] for n, at in enumerate(near)}
    start = [jump_at(load_tiles, a, 0, lookups[a]) for a in range(2)]
    publish(0, start, [multiply(start[a], lpair[a]) for a in range(2)], None)

    arrived(SIDE)
    arrived(FLAT)
    arrived(DIRICH)

    def edge_into(block, a, s, first):
        high, low = split(block.T)
        fpair[a, s * width : (s + 1) * width, first : first + edge] = high
        fpair[a, s * width : (s + 1) * width, width + first : width + first + edge] = low

    for a in range(2):
        split_into(dpair.at[a], [dbuf[a, s] for s in range(sc)])
        edge_into(dside[a], a, 0, edge * (1 - (a + sc - 1) % 2))
        edge_into(dside[2 + a], a, sc - 1, edge * (a % 2))
        for s in range(sc):
            edge_into(dflat[a, s], a, s, edge * (2 + s % 2))

    group = nrhs // sc
    order = list(keys)
    nothing = jnp.zeros((rows, width), jnp.float32)
    batches = [order[first : first + group] for first in range(0, len(order), group)]
    basis_images = []
    for batch in batches:
        tiles = {at: nothing for at in order}
        for g, at in enumerate(batch):
            tiles[at] = jnp.where(rhs_row == g * sc + sub_row, couplings[at], 0.0)
        basis_images.append(images_of(tiles))
    stacked = {at: jnp.concatenate([images[at] for images in basis_images], axis=0) for at in basis_images[0]}
    basis_weighted = precondition(stacked)
    stacked_steps = []
    for a in range(2):
        parts = [
            jump_at({at: basis_weighted[a][at][b * rows : (b + 1) * rows] for at in basis_weighted[a]}, a, 0, lookups[a])
            for b in range(len(batches))
        ]
        stacked_steps.append(jnp.concatenate(parts, axis=0))
    stacked_u = [multiply(2.0 * stacked_steps[a], lpair[a]) for a in range(2)]

    def table_of(stacks, farthest):
        tables = []
        for a, stack in enumerate(stacks):
            table = {}
            for n, at in enumerate(order):
                if reach(a, at) > farthest:
                    continue
                first = (n // group) * rows + (n % group) * sc
                for m in range(sc):
                    value = None
                    for s in range(sc):
                        at_row = first + s * nrhs + (s - m) % sc
                        line = jnp.broadcast_to(stack[at_row : at_row + 1], (rows, width))
                        value = line if value is None else jnp.where(sub_row == s, line, value)
                    table[at, m] = value
            tables.append(table)
        return tables

    image_table = table_of([stacked[key(a, 0)] for a in range(2)], 1)
    step_table = table_of(stacked_steps, 2)
    u_table = table_of(stacked_u, 2)

    arrived(KROW)

    def widen(k):
        kt[k] = jnp.where(of_rhs, spread(kc[k]), 0.0)

    if ndev <= UNROLL:
        for k in range(ndev):
            widen(k)
    else:
        pl.loop(0, ndev)(widen)

    def pairwise(function, *operands):
        return [function(*(operand[a] for operand in operands)) for a in range(2)]

    image, step, lifted = advance(collect_tiles(0), True)
    turned, _, _ = collect_sums(0, False)
    residual = coarse(image, image_table, turned)
    precon = coarse(step, step_table, turned)
    u = coarse(lifted, u_table, turned)

    multipliers = [nothing, nothing]
    search = along = steps = lifts = gamma = step_size = None
    for iteration in range(ITERS):
        rd = iteration + 1
        last = rd == ITERS
        doubled = [2.0 * value for value in precon]
        dots = (residual[0] * precon[0] + residual[1] * precon[1], doubled[0] * u[0] + doubled[1] * u[1])
        publish(rd, doubled, u, dots)
        if iteration == 0:
            for what in arrivals:
                left(what)
        sent(rd - 1)
        if last:
            sent(rd)
        image, step, lifted = advance(collect_tiles(rd), not last)
        turned, gamma_new, curve = collect_sums(rd, True)
        image = coarse(image, image_table, turned)
        if not last:
            step = coarse(step, step_table, turned)
            lifted = coarse(lifted, u_table, turned)
        if iteration == 0:
            step_size = gamma_new / curve
            search, along, steps, lifts = precon, image, step, lifted
        else:
            ratio = gamma_new / gamma
            step_size = gamma_new / (curve - ratio * gamma_new / step_size)
            search = pairwise(lambda new, old: new + ratio * old, precon, search)
            along = pairwise(lambda new, old: new + ratio * old, image, along)
            if not last:
                steps = pairwise(lambda new, old: new + ratio * old, step, steps)
                lifts = pairwise(lambda new, old: new + ratio * old, lifted, lifts)
        gamma = gamma_new
        multipliers = pairwise(lambda value, move: value + step_size * move, multipliers, search)
        residual = pairwise(lambda value, move: value - step_size * move, residual, along)
        if not last:
            precon = pairwise(lambda value, move: value - step_size * move, precon, steps)
            u = pairwise(lambda value, move: value - step_size * move, u, lifts)
    first_row = jnp.full((rows, width), core, jnp.int32) == 0
    out[0] = pick(jnp.where(first_row, multipliers[0], multipliers[1]), backward)
    out[1] = pick(jnp.where(first_row, residual[0], residual[1]), backward)


def solution(mesh):
    nr, nc = mesh.shape["srow"], mesh.shape["scol"]
    slots = block_slots(nr // 2, nc)

    def body(loads, local_inverse, dirichlet, corner_coupling, coarse_inverse, partner):
        sr, sc, nrhs, width = loads.shape
        rows = sr * sc * nrhs
        ndev = nr * nc
        lanes = -(-(nrhs * nc * sc + 2 * nrhs) // 128) * 128
        dma = pltpu.SemaphoreType.DMA
        f32 = jnp.float32
        vmem = pl.BlockSpec(memory_space=pltpu.VMEM)
        hbm = pl.BlockSpec(memory_space=pl.ANY)
        rounds = ITERS + 1
        edge = width // 4
        out = pl.pallas_call(
            functools.partial(kernel, nr, nc, slots, sc, nrhs),
            out_shape=pltpu.VMEM((2, rows, width), f32),
            in_specs=[hbm] * 6,
            out_specs=vmem,
            scratch_shapes=[
                pltpu.VMEM((sc, coarse_inverse.shape[-1]), f32),
                pltpu.VMEM((rows, width), f32),
                pltpu.VMEM((sc, width), f32),
                pltpu.VMEM((sc, width), jnp.int32),
                pltpu.VMEM((2, sc, width, width), f32),
                pltpu.VMEM((2, sc, width, width), f32),
                pltpu.VMEM((2, sc * width, 2 * width), jnp.bfloat16),
                pltpu.VMEM((2, sc * width, 2 * width), jnp.bfloat16),
                pltpu.VMEM((2, sc * width, 2 * width), jnp.bfloat16),
                pltpu.VMEM((8, rows, width), f32),
                pltpu.VMEM((8, sc, width), f32),
                pltpu.VMEM((2 * len(slots), sc, width), f32),
                pltpu.VMEM((4, edge, width), f32),
                pltpu.VMEM((2, sc, edge, width), f32),
                pltpu.VMEM((ndev, sc, lanes), f32),
                pltpu.VMEM((ndev, rows, lanes), f32),
                pltpu.VMEM((rounds, len(slots), 2, rows, width), f32),
                pltpu.VMEM((rounds, ndev // 2, 2, lanes), f32),
                dma((6,)), dma((8,)), dma((8,)),
                dma((rounds,)), dma((rounds,)),
                dma((rounds,)), dma((rounds,)),
            ],
            compiler_params=pltpu.CompilerParams(collective_id=0, has_side_effects=True),
        )(
            loads.reshape(rows, width),
            corner_coupling.reshape(sc, width),
            coarse_inverse.reshape(sc, coarse_inverse.shape[-1]),
            partner.reshape(sc, width),
            local_inverse.reshape(sc, width, width),
            dirichlet.reshape(sc, width, width),
        )
        return out[0].reshape(loads.shape), out[1].reshape(loads.shape)

    whole, lists = P("srow", "scol", None, None), P("srow", "scol", None)
    return jax.shard_map(
        body,
        mesh=mesh,
        in_specs=(whole, whole, whole, lists, lists, lists),
        out_specs=(whole, whole),
        check_vma=False,
    )
```

time: 31.7 us -> 29.8 us (0.940)
  Pallas kernels: 30.3 us -> 28.4 us
    pallas_call x1, Pallas kernels: 30.3 us -> 28.4 us  [body(): pl.pallas_call(functools.partial(kernel, nr, nc, slots, sc, nrhs), out_sh...]
where the time goes in v2:
time: 29.8 us; the launch traced here: 29.6 us
  Pallas kernels  28.4 us (95%)
  between operations  0.64 us (2%)
  local copies, waits for them, and re-layouts  0.6 us (2%)
    pallas_call x1, Pallas kernels, body(): pl.pallas_call(functools.partial(kernel, nr, nc, slots, sc, nrhs), out_sh...  28.4 us
    slice x1, local copies, waits for them, and re-layouts, body(): return (out[0].reshape(loads.shape), out[1].reshape(loads.shape))  0.6 us

profile of v2, /device:TPU:0, one launch (start us, length us, event | category | flops | bytes accessed | tf_op | source)
XLA Modules:
  0.0 29.6 jit_solution(14077760083215054636)
XLA Ops:
  0.6 28.4 %shard_map.77 = f32[2,8,128]{2,1,0:T(8,128)S(1)} custom-call(f32[8,128]{1,0:T(8,128)} %bitcast.10, f32[2,128]{1,0:T(2,128)} %bitcast.13, f32[2,16]{1,0:T(2,128)} %bitcast.14, s32[2,128]{1,0:T(2,128)} %bitcast.15, f32[2,128,128]{2,1,0:T(8,128)} %bitcast.8, f32[2,128,128]{2,1,0:T(8,128)} %bitcast.9), custom_call_target="tpu_custom_call" | custom-call | tf_op jit(solution)/shard_map/pallas_call | solution.py:529
  29.0 0.6 %fusion = (f32[1,8,128]{2,1,0:T(8,128)}, f32[1,8,128]{2,1,0:T(8,128)}) fusion(f32[2,8,128]{2,1,0:T(8,128)S(1)} %shard_map.77), kind=kLoop, calls=%fused_computation | loop fusion | bytes 16384 | tf_op jit(solution)/shard_map/slice | solution.py:566

commit v3 on v2

--- a/solution.py
+++ b/solution.py
@@ -38,10 +38,27 @@
     near = [(0, 0), (1, 0), (0, 1), (1, 1), (0, nc - 1), (1, nc - 1), (nr - 1, 0), (2, 0)]
     LOADS, PART, CPL, LINV, DIRICH, SIDE, FLAT, KROW = range(8)
 
+    def flip(index, mask):
+        for bit in range(mask.bit_length()):
+            if mask >> bit & 1:
+                index = index + (1 << bit) - (2 << bit) * lax.rem(lax.div(index, 1 << bit), 2)
+        return index
+
+    powers = nb & (nb - 1) == 0 and nc & (nc - 1) == 0
+    masks = sorted(((a, b) for a in range(nb) for b in range(nc) if a or b), key=lambda m: -(m[0] + m[1] // 2 + m[1] % 2))
+
+    paired = ndev <= UNROLL and powers
+    rows_to = [flip(i, 2 * a + c) for a in range(nb) for c in range(2)] if paired else []
+    cols_to = [flip(j, b) for b in range(nc)] if paired else []
+
     def others(step):
-        if ndev <= UNROLL:
-            far_first = sorted(range(1, ndev), key=lambda k: (-min(k // nc, nr - k // nc), min(k % nc, nc - k % nc) % (nc // 2)))
-            for k in far_first:
+        if paired:
+            for a, b in [*masks, (0, 0)]:
+                for c in range(2):
+                    if a or b or c:
+                        step(rows_to[2 * a + c], cols_to[b])
+        elif ndev <= UNROLL:
+            for k in range(1, ndev):
                 step(lax.rem(i + k // nc, nr), lax.rem(j + k % nc, nc))
         else:
             @pl.loop(1, ndev)
@@ -53,16 +70,17 @@
     def greet(ti, tj):
         pl.semaphore_signal(barrier, inc=1, device_id=(ti, tj), device_id_type=MESH)
 
-    others(greet)
-
     fetches = [
         pltpu.make_async_copy(src, dst, local_sem.at[n])
         for n, (src, dst) in enumerate((
-            (cinv_in, cinv), (loads_in, loads), (cpl_in, cpl), (part_in, part),
+            (loads_in, loads), (part_in, part), (cpl_in, cpl), (cinv_in, cinv),
             (linv, lbuf.at[core]), (dirich, dbuf.at[core]),
         ))
     ]
-    for fetch in fetches:
+    for fetch in fetches[:2]:
+        fetch.start()
+    others(greet)
+    for fetch in fetches[2:]:
         fetch.start()
 
     row = lax.broadcasted_iota(jnp.int32, (rows, width), 0)
@@ -107,15 +125,8 @@
             pair[s * width : (s + 1) * width, 0:width] = high
             pair[s * width : (s + 1) * width, width : 2 * width] = low
 
-    tile_lane = lax.broadcasted_iota(jnp.int32, (ncols, lanes), 1)
-    tile_row = lax.broadcasted_iota(jnp.int32, (ncols, lanes), 0)
-    tiler = jnp.where(lax.rem(tile_lane, ncols) == tile_row, 1.0, 0.0)
-    for fetch in fetches[:4]:
+    for fetch in fetches[:2]:
         fetch.wait()
-    tiled = jnp.dot(spread(cinv[...]), tiler, precision=precise, preferred_element_type=jnp.float32)
-    for s in range(sc):
-        kc[core * nc, s : s + 1] = tiled[s * nrhs : s * nrhs + 1]
-    own_place = place(0)
     partner = spread(part[...])
     other = edge * (1 - 2 * half)
     mirrored = jnp.where((half == 1) & (partner >= 0), partner + side * edge, lane)
@@ -125,10 +136,8 @@
     backward = jnp.where(own_odd == 1, mirrored + other, mirrored)
     loads_n[core] = pick(loads[...], forward)
     active_own = pick(jnp.where(partner >= 0, 1.0, 0.0), forward)
-    coupling_own = pick(spread(cpl[...]), forward)
     for s in range(sc):
         part_n[core, s : s + 1] = active_own[s * nrhs : s * nrhs + 1]
-        cpl_n[core, s : s + 1] = coupling_own[s * nrhs : s * nrhs + 1]
 
     def reorder(buffer):
         for s in range(sc):
@@ -152,6 +161,10 @@
         push(loads_n.at[core], loads_n.at[n], LOADS, ti, tj)
     for n, ti, tj in toward:
         push(part_n.at[core], part_n.at[n], PART, ti, tj)
+    fetches[2].wait()
+    coupling_own = pick(spread(cpl[...]), forward)
+    for s in range(sc):
+        cpl_n[core, s : s + 1] = coupling_own[s * nrhs : s * nrhs + 1]
     for n, (dp, dj) in enumerate(slots):
         for t in range(2):
             ti, tj = 2 * lax.rem(p - dp + nb, nb) + t, lax.rem(j - dj + nc, nc)
@@ -160,6 +173,14 @@
                     push(cpl_n.at[core], cpl_n.at[core], CPL, partner_i, j)
             else:
                 push(cpl_n.at[core], cpl_n.at[2 * n + core], CPL, ti, tj)
+    tile_lane = lax.broadcasted_iota(jnp.int32, (ncols, lanes), 1)
+    tile_row = lax.broadcasted_iota(jnp.int32, (ncols, lanes), 0)
+    tiler = jnp.where(lax.rem(tile_lane, ncols) == tile_row, 1.0, 0.0)
+    fetches[3].wait()
+    tiled = jnp.dot(spread(cinv[...]), tiler, precision=precise, preferred_element_type=jnp.float32)
+    for s in range(sc):
+        kc[core * nc, s : s + 1] = tiled[s * nrhs : s * nrhs + 1]
+    own_place = place(0)
     def send_k(ti, tj):
         slot = lax.rem(i - 2 * lax.div(ti, 2) + nr, nr) * nc + lax.rem(j - tj + nc, nc)
         push(kc.at[core * nc], kc.at[slot], KROW, ti, tj)
@@ -217,8 +238,8 @@
 
     def multiply(values, pair):
         total = values.shape[0]
-        high, low = split(values)
-        stacked = jnp.concatenate([high.astype(jnp.float32), low.astype(jnp.float32)], axis=0)
+        high = values.astype(jnp.bfloat16).astype(jnp.float32)
+        stacked = jnp.concatenate([high, values - high], axis=0)
         sub = lax.rem(lax.div(lax.broadcasted_iota(jnp.int32, stacked.shape, 0), nrhs), sc)
         wide = jnp.concatenate([jnp.where(sub == s, stacked, 0.0) for s in range(sc)], axis=1)
         product = jnp.dot(wide.astype(jnp.bfloat16), pair, preferred_element_type=jnp.float32)
@@ -231,15 +252,6 @@
 
     def reach(a, at):
         return min((at[0] - a) % nr, (a - at[0]) % nr) + min(at[1], nc - at[1])
-
-    def flip(index, mask):
-        for bit in range(mask.bit_length()):
-            if mask >> bit & 1:
-                index = index + (1 << bit) - (2 << bit) * lax.rem(lax.div(index, 1 << bit), 2)
-        return index
-
-    powers = nb & (nb - 1) == 0 and nc & (nc - 1) == 0
-    masks = sorted(((a, b) for a in range(nb) for b in range(nc) if a or b), key=lambda m: -(m[0] + m[1] // 2 + m[1] % 2))
 
     def q_target(tp, tj):
         return lax.rem(p - tp + nb, nb) * nc + lax.rem(j - tj + nc, nc), 2 * tp + 1 - core, tj
@@ -289,11 +301,11 @@
     def collect_tiles(rd):
         bytes_u = ub.at[rd, pl.ds(1, len(slots) - 1)]
         pltpu.make_async_copy(bytes_u, bytes_u, u_recv.at[rd]).wait()
+        return {at: ub[rd, n, a] for at, (n, a) in keys.items()}
+
+    def collect_sums(rd, want_dots):
         bytes_q = qb.at[rd, pl.ds(1, nblocks - 1)]
         pltpu.make_async_copy(bytes_q, bytes_q, q_recv.at[rd]).wait()
-        return {at: ub[rd, n, a] for at, (n, a) in keys.items()}
-
-    def collect_sums(rd, want_dots):
         sums = [jnp.sum(qb[rd, pl.ds(d * nc, nc)], axis=0) for d in range(nb)]
         band = [jnp.broadcast_to(sums[d // 2][d % 2 : d % 2 + 1], (rows, lanes)) for d in range(nr)]
         cols = {}
@@ -335,11 +347,11 @@
         weighted = []
         for a in range(2):
             total = images[key(a, 0)].shape[0]
-            ring = multiply(2.0 * jnp.concatenate([images[at] for at in beside(a)], axis=0), fpair[a])
+            ring = multiply(jnp.concatenate([images[at] for at in beside(a)], axis=0), fpair[a])
             weighted.append({at: ring[m * total : (m + 1) * total] for m, at in enumerate(beside(a))})
             weighted[a][key(a, -1)] = weighted[a][key(a, 1)]
         for a in range(2):
-            mine = multiply(2.0 * images[key(a, 0)], dpair[a])
+            mine = multiply(images[key(a, 0)], dpair[a])
             for ring in weighted:
                 ring[key(a, 0)] = mine
         return weighted
@@ -359,24 +371,27 @@
 
     def advance(tiles, keep):
         if not keep:
-            return [jump_at(tiles, a, 0, lookups[a]) for a in range(2)], None, None
+            return [jump_at(tiles, a, 0, lookups[a]) for a in range(2)], None
         images = images_of(tiles)
         weighted = precondition(images)
         step = [jump_at(weighted[a], a, 0, lookups[a]) for a in range(2)]
-        return [images[key(a, 0)] for a in range(2)], step, [multiply(2.0 * step[a], lpair[a]) for a in range(2)]
-
-    def coarse(base, table, turned):
-        out = []
+        return [images[key(a, 0)] for a in range(2)], step
+
+    def lift(step):
+        return [multiply(step[a], lpair[a]) for a in range(2)]
+
+    def coarse(table, turned):
+        sums = []
         for a in range(2):
-            value = base[a]
-            for at, m in table[a]:
-                value = value + table[a][at, m] * turned[at, m]
-            out.append(value)
-        return out
+            terms = [table[a][at, m] * turned[at, m] for at, m in table[a]]
+            while len(terms) > 1:
+                terms = [sum(terms[k + 1 : k + 2], terms[k]) for k in range(0, len(terms), 2)]
+            sums.append(terms[0])
+        return sums
 
     arrived(LINV)
     for a in range(2):
-        split_into(lpair.at[a], [lbuf[a, s] for s in range(sc)])
+        split_into(lpair.at[a], [2.0 * lbuf[a, s] for s in range(sc)])
         fpair[a] = jnp.zeros(fpair.shape[1:], jnp.bfloat16)
 
     arrived(PART)
@@ -388,19 +403,19 @@
     arrived(LOADS)
     load_tiles = {key(*at): loads_n[n] for n, at in enumerate(near)}
     start = [jump_at(load_tiles, a, 0, lookups[a]) for a in range(2)]
-    publish(0, start, [multiply(start[a], lpair[a]) for a in range(2)], None)
+    publish(0, start, [multiply(0.5 * start[a], lpair[a]) for a in range(2)], None)
 
     arrived(SIDE)
     arrived(FLAT)
     arrived(DIRICH)
 
     def edge_into(block, a, s, first):
-        high, low = split(block.T)
+        high, low = split(2.0 * block.T)
         fpair[a, s * width : (s + 1) * width, first : first + edge] = high
         fpair[a, s * width : (s + 1) * width, width + first : width + first + edge] = low
 
     for a in range(2):
-        split_into(dpair.at[a], [dbuf[a, s] for s in range(sc)])
+        split_into(dpair.at[a], [2.0 * dbuf[a, s] for s in range(sc)])
         edge_into(dside[a], a, 0, edge * (1 - (a + sc - 1) % 2))
         edge_into(dside[2 + a], a, sc - 1, edge * (a % 2))
         for s in range(sc):
@@ -425,7 +440,7 @@
             for b in range(len(batches))
         ]
         stacked_steps.append(jnp.concatenate(parts, axis=0))
-    stacked_u = [multiply(2.0 * stacked_steps[a], lpair[a]) for a in range(2)]
+    stacked_u = [multiply(stacked_steps[a], lpair[a]) for a in range(2)]
 
     def table_of(stacks, farthest):
         tables = []
@@ -463,14 +478,18 @@
     def pairwise(function, *operands):
         return [function(*(operand[a] for operand in operands)) for a in range(2)]
 
-    image, step, lifted = advance(collect_tiles(0), True)
+    def plus(left, right):
+        return pairwise(jnp.add, left, right)
+
+    image, step = advance(collect_tiles(0), True)
     turned, _, _ = collect_sums(0, False)
-    residual = coarse(image, image_table, turned)
-    precon = coarse(step, step_table, turned)
-    u = coarse(lifted, u_table, turned)
+    lifted = lift(step)
+    residual = plus(image, coarse(image_table, turned))
+    precon = plus(step, coarse(step_table, turned))
+    u = plus(lifted, coarse(u_table, turned))
 
     multipliers = [nothing, nothing]
-    search = along = steps = lifts = gamma = step_size = None
+    search = along = steps = lifts = gamma = step_size = ratio = None
     for iteration in range(ITERS):
         rd = iteration + 1
         last = rd == ITERS
@@ -483,29 +502,36 @@
         sent(rd - 1)
         if last:
             sent(rd)
-        image, step, lifted = advance(collect_tiles(rd), not last)
+        image, step = advance(collect_tiles(rd), not last)
         turned, gamma_new, curve = collect_sums(rd, True)
-        image = coarse(image, image_table, turned)
-        if not last:
-            step = coarse(step, step_table, turned)
-            lifted = coarse(lifted, u_table, turned)
         if iteration == 0:
             step_size = gamma_new / curve
-            search, along, steps, lifts = precon, image, step, lifted
+            search = precon
         else:
             ratio = gamma_new / gamma
             step_size = gamma_new / (curve - ratio * gamma_new / step_size)
             search = pairwise(lambda new, old: new + ratio * old, precon, search)
-            along = pairwise(lambda new, old: new + ratio * old, image, along)
-            if not last:
-                steps = pairwise(lambda new, old: new + ratio * old, step, steps)
-                lifts = pairwise(lambda new, old: new + ratio * old, lifted, lifts)
+
+        def known(table, old):
+            fixed = coarse(table, turned)
+            return fixed if old is None else pairwise(lambda new, before: new + ratio * before, fixed, old)
+
+        def descend(value, fixed, new):
+            return pairwise(lambda v, f, n: (v - step_size * f) - step_size * n, value, fixed, new)
+
         gamma = gamma_new
         multipliers = pairwise(lambda value, move: value + step_size * move, multipliers, search)
-        residual = pairwise(lambda value, move: value - step_size * move, residual, along)
+        fixed = known(image_table, along)
+        residual = descend(residual, fixed, image)
+        along = plus(image, fixed)
         if not last:
-            precon = pairwise(lambda value, move: value - step_size * move, precon, steps)
-            u = pairwise(lambda value, move: value - step_size * move, u, lifts)
+            fixed = known(step_table, steps)
+            precon = descend(precon, fixed, step)
+            steps = plus(step, fixed)
+            fixed = known(u_table, lifts)
+            lifted = lift(step)
+            u = descend(u, fixed, lifted)
+            lifts = plus(lifted, fixed)
     first_row = jnp.full((rows, width), core, jnp.int32) == 0
     out[0] = pick(jnp.where(first_row, multipliers[0], multipliers[1]), backward)
     out[1] = pick(jnp.where(first_row, residual[0], residual[1]), backward)

time: 29.8 us -> 29.3 us (0.983)
  Pallas kernels: 28.4 us -> 27.9 us
    pallas_call x1, Pallas kernels: 28.4 us -> 27.9 us  [body(): pl.pallas_call(functools.partial(kernel, nr, nc, slots, sc, nrhs), out_sh...]
where the time goes in v3:
time: 29.3 us; the launch traced here: 29.1 us
  Pallas kernels  27.9 us (95%)
  between operations  0.64 us (2%)
  local copies, waits for them, and re-layouts  0.6 us (2%)
    pallas_call x1, Pallas kernels, body(): pl.pallas_call(functools.partial(kernel, nr, nc, slots, sc, nrhs), out_sh...  27.9 us
    slice x1, local copies, waits for them, and re-layouts, body(): return (out[0].reshape(loads.shape), out[1].reshape(loads.shape))  0.6 us

profile of v3, /device:TPU:0, one launch (start us, length us, event | category | flops | bytes accessed | tf_op | source)
XLA Modules:
  0.0 29.1 jit_solution(2448178901140707128)
XLA Ops:
  0.6 27.9 %shard_map.77 = f32[2,8,128]{2,1,0:T(8,128)S(1)} custom-call(f32[8,128]{1,0:T(8,128)} %bitcast.10, f32[2,128]{1,0:T(2,128)} %bitcast.13, f32[2,16]{1,0:T(2,128)} %bitcast.14, s32[2,128]{1,0:T(2,128)} %bitcast.15, f32[2,128,128]{2,1,0:T(8,128)} %bitcast.8, f32[2,128,128]{2,1,0:T(8,128)} %bitcast.9), custom_call_target="tpu_custom_call" | custom-call | tf_op jit(solution)/shard_map/pallas_call | solution.py:555
  28.5 0.6 %fusion = (f32[1,8,128]{2,1,0:T(8,128)}, f32[1,8,128]{2,1,0:T(8,128)}) fusion(f32[2,8,128]{2,1,0:T(8,128)S(1)} %shard_map.77), kind=kLoop, calls=%fused_computation | loop fusion | bytes 16384 | tf_op jit(solution)/shard_map/slice | solution.py:592

commit v4 on v3

--- a/solution.py
+++ b/solution.py
@@ -36,7 +36,7 @@
     i, j = lax.axis_index("srow"), lax.axis_index("scol")
     p, core = lax.div(i, 2), lax.rem(i, 2)
     near = [(0, 0), (1, 0), (0, 1), (1, 1), (0, nc - 1), (1, nc - 1), (nr - 1, 0), (2, 0)]
-    LOADS, PART, CPL, LINV, DIRICH, SIDE, FLAT, KROW = range(8)
+    LOADS, PART, CPL, LINV, DIRICH, SIDE, FLAT, KROW, PAIR_PART, PAIR_CPL = range(10)
 
     def flip(index, mask):
         for bit in range(mask.bit_length()):
@@ -159,19 +159,18 @@
     toward = around + [(core, partner_i, j)]
     for n, ti, tj in toward:
         push(loads_n.at[core], loads_n.at[n], LOADS, ti, tj)
-    for n, ti, tj in toward:
+    push(part_n.at[core], part_n.at[core], PAIR_PART, partner_i, j)
+    for n, ti, tj in around:
         push(part_n.at[core], part_n.at[n], PART, ti, tj)
     fetches[2].wait()
     coupling_own = pick(spread(cpl[...]), forward)
     for s in range(sc):
         cpl_n[core, s : s + 1] = coupling_own[s * nrhs : s * nrhs + 1]
+    push(cpl_n.at[core], cpl_n.at[core], PAIR_CPL, partner_i, j)
     for n, (dp, dj) in enumerate(slots):
         for t in range(2):
             ti, tj = 2 * lax.rem(p - dp + nb, nb) + t, lax.rem(j - dj + nc, nc)
-            if (dp, dj) == (0, 0):
-                if t == 0:
-                    push(cpl_n.at[core], cpl_n.at[core], CPL, partner_i, j)
-            else:
+            if n:
                 push(cpl_n.at[core], cpl_n.at[2 * n + core], CPL, ti, tj)
     tile_lane = lax.broadcasted_iota(jnp.int32, (ncols, lanes), 1)
     tile_row = lax.broadcasted_iota(jnp.int32, (ncols, lanes), 0)
@@ -205,7 +204,8 @@
     push(dbuf.at[core], dbuf.at[core], DIRICH, partner_i, j)
 
     arrivals = {
-        LOADS: loads_n.at[pl.ds(0, 7)], PART: part_n.at[pl.ds(0, 7)], CPL: cpl_n.at[pl.ds(0, 2 * len(slots) - 1)],
+        LOADS: loads_n.at[pl.ds(0, 7)], PART: part_n.at[pl.ds(0, 6)], CPL: cpl_n.at[pl.ds(0, 2 * len(slots) - 2)],
+        PAIR_PART: part_n.at[0], PAIR_CPL: cpl_n.at[0],
         LINV: lbuf.at[0], DIRICH: dbuf.at[0], SIDE: dside, FLAT: dflat, KROW: kc.at[pl.ds(0, ndev - 1)],
     }
 
@@ -394,17 +394,24 @@
         split_into(lpair.at[a], [2.0 * lbuf[a, s] for s in range(sc)])
         fpair[a] = jnp.zeros(fpair.shape[1:], jnp.bfloat16)
 
-    arrived(PART)
-    partners = [spread(part_n[n]) for n in range(len(near))]
+    arrived(PAIR_PART)
+    arrived(PAIR_CPL)
+    partners = [spread(part_n[n]) for n in range(2)]
     lookups = [partner > 0.5 for partner in partners]
-    side_lookups = [jnp.where(row < nrhs, partners[EAST + a], partners[WEST + a]) > 0.5 for a in range(2)]
-    arrived(CPL)
-    couplings = {at: spread(cpl_n[2 * n + a]) for at, (n, a) in keys.items()}
+    couplings = {(a, 0): spread(cpl_n[a]) for a in range(2)}
     arrived(LOADS)
     load_tiles = {key(*at): loads_n[n] for n, at in enumerate(near)}
     start = [jump_at(load_tiles, a, 0, lookups[a]) for a in range(2)]
     publish(0, start, [multiply(0.5 * start[a], lpair[a]) for a in range(2)], None)
 
+    arrived(PART)
+    partners += [spread(part_n[n]) for n in range(2, len(near))]
+    lookups += [partner > 0.5 for partner in partners[2:]]
+    side_lookups = [jnp.where(row < nrhs, partners[EAST + a], partners[WEST + a]) > 0.5 for a in range(2)]
+    arrived(CPL)
+    for at, (n, a) in keys.items():
+        if n:
+            couplings[at] = spread(cpl_n[2 * n + a])
     arrived(SIDE)
     arrived(FLAT)
     arrived(DIRICH)
@@ -576,7 +583,7 @@
                 pltpu.VMEM((ndev, rows, lanes), f32),
                 pltpu.VMEM((rounds, len(slots), 2, rows, width), f32),
                 pltpu.VMEM((rounds, ndev // 2, 2, lanes), f32),
-                dma((6,)), dma((8,)), dma((8,)),
+                dma((6,)), dma((10,)), dma((10,)),
                 dma((rounds,)), dma((rounds,)),
                 dma((rounds,)), dma((rounds,)),
             ],

time: 29.3 us -> 29.2 us (level)
  no operation moved by 1% of the time
where the time goes in v4:
time: 29.2 us; the launch traced here: 29 us
  Pallas kernels  27.7 us (95%)
  between operations  0.64 us (2%)
  local copies, waits for them, and re-layouts  0.6 us (2%)
    pallas_call x1, Pallas kernels, body(): pl.pallas_call(functools.partial(kernel, nr, nc, slots, sc, nrhs), out_sh...  27.7 us
    slice x1, local copies, waits for them, and re-layouts, body(): return (out[0].reshape(loads.shape), out[1].reshape(loads.shape))  0.6 us

profile of v4, /device:TPU:0, one launch (start us, length us, event | category | flops | bytes accessed | tf_op | source)
XLA Modules:
  0.0 29.0 jit_solution(5909911206307172149)
XLA Ops:
  0.6 27.7 %shard_map.77 = f32[2,8,128]{2,1,0:T(8,128)S(1)} custom-call(f32[8,128]{1,0:T(8,128)} %bitcast.10, f32[2,128]{1,0:T(2,128)} %bitcast.13, f32[2,16]{1,0:T(2,128)} %bitcast.14, s32[2,128]{1,0:T(2,128)} %bitcast.15, f32[2,128,128]{2,1,0:T(8,128)} %bitcast.8, f32[2,128,128]{2,1,0:T(8,128)} %bitcast.9), custom_call_target="tpu_custom_call" | custom-call | tf_op jit(solution)/shard_map/pallas_call | solution.py:562
  28.4 0.6 %fusion = (f32[1,8,128]{2,1,0:T(8,128)}, f32[1,8,128]{2,1,0:T(8,128)}) fusion(f32[2,8,128]{2,1,0:T(8,128)S(1)} %shard_map.77), kind=kLoop, calls=%fused_computation | loop fusion | bytes 16384 | tf_op jit(solution)/shard_map/slice | solution.py:599

commit v5 on v4

--- a/solution.py
+++ b/solution.py
@@ -16,7 +16,7 @@
 
 def block_slots(nb, nc):
     slots = []
-    for dp, dj in ((0, 0), (0, 1), (0, -1), (1, 1), (1, -1), (-1, 1), (-1, -1), (1, 0), (-1, 0)):
+    for dp, dj in ((0, 0), (0, 1), (0, -1), (1, 0), (-1, 0), (1, 1), (1, -1), (-1, 1), (-1, -1)):
         off = (dp % nb, dj % nc)
         if off not in slots:
             slots.append(off)
@@ -274,7 +274,7 @@
                 src_ref=src, dst_ref=dst, send_sem=send.at[rd], recv_sem=recv.at[rd],
                 device_id=(ti, tj), device_id_type=MESH).start()
 
-        for n, ti, tj in u_targets:
+        for n, ti, tj in [target for target in u_targets if target[0] < reached(rd)]:
             across(ub.at[rd, 0], ub.at[rd, n], u_send, u_recv, ti, tj)
         for a in range(2):
             message = jnp.where(own_place, lane_sum(couplings[a, 0] * values[a]), 0.0)
@@ -292,16 +292,21 @@
                 slot, ti, tj = q_target(lax.rem(p + lax.div(k, nc), nb), lax.rem(j + lax.rem(k, nc), nc))
                 across(qb.at[rd, 0], qb.at[rd, slot], q_send, q_recv, ti, tj)
 
+    straight = sum(1 for dp, dj in slots if not dp or not dj)
+
+    def reached(rd):
+        return straight if rd == ITERS else len(slots)
+
     def sent(rd):
         bytes_q = qb.at[rd, pl.ds(1, nblocks - 1)]
         pltpu.make_async_copy(bytes_q, bytes_q, q_send.at[rd]).wait()
-        bytes_u = ub.at[rd, pl.ds(1, len(slots) - 1)]
+        bytes_u = ub.at[rd, pl.ds(1, reached(rd) - 1)]
         pltpu.make_async_copy(bytes_u, bytes_u, u_send.at[rd]).wait()
 
     def collect_tiles(rd):
-        bytes_u = ub.at[rd, pl.ds(1, len(slots) - 1)]
+        bytes_u = ub.at[rd, pl.ds(1, reached(rd) - 1)]
         pltpu.make_async_copy(bytes_u, bytes_u, u_recv.at[rd]).wait()
-        return {at: ub[rd, n, a] for at, (n, a) in keys.items()}
+        return {at: ub[rd, n, a] for at, (n, a) in keys.items() if n < reached(rd)}
 
     def collect_sums(rd, want_dots):
         bytes_q = qb.at[rd, pl.ds(1, nblocks - 1)]
@@ -495,6 +500,11 @@
     precon = plus(step, coarse(step_table, turned))
     u = plus(lifted, coarse(u_table, turned))
 
+    first_row = jnp.full((rows, width), core, jnp.int32) == 0
+
+    def placed(values):
+        return pick(jnp.where(first_row, values[0], values[1]), backward)
+
     multipliers = [nothing, nothing]
     search = along = steps = lifts = gamma = step_size = ratio = None
     for iteration in range(ITERS):
@@ -517,6 +527,7 @@
         else:
             ratio = gamma_new / gamma
             step_size = gamma_new / (curve - ratio * gamma_new / step_size)
+            old_search = search
             search = pairwise(lambda new, old: new + ratio * old, precon, search)
 
         def known(table, old):
@@ -527,6 +538,14 @@
             return pairwise(lambda v, f, n: (v - step_size * f) - step_size * n, value, fixed, new)
 
         gamma = gamma_new
+        if last:
+            move = placed(precon) if ratio is None else placed(precon) + ratio * placed(old_search)
+            out[0] = placed(multipliers) + step_size * move
+            fixed = placed(coarse(image_table, turned))
+            if ratio is not None:
+                fixed = fixed + ratio * placed(along)
+            out[1] = (placed(residual) - step_size * fixed) - step_size * placed(image)
+            break
         multipliers = pairwise(lambda value, move: value + step_size * move, multipliers, search)
         fixed = known(image_table, along)
         residual = descend(residual, fixed, image)
@@ -539,9 +558,6 @@
             lifted = lift(step)
             u = descend(u, fixed, lifted)
             lifts = plus(lifted, fixed)
-    first_row = jnp.full((rows, width), core, jnp.int32) == 0
-    out[0] = pick(jnp.where(first_row, multipliers[0], multipliers[1]), backward)
-    out[1] = pick(jnp.where(first_row, residual[0], residual[1]), backward)
 
 
 def solution(mesh):

time: 29.2 us -> 29 us (level)
  no operation moved by 1% of the time
where the time goes in v5:
time: 29 us; the launch traced here: 28.8 us
  Pallas kernels  27.6 us (95%)
  between operations  0.64 us (2%)
  local copies, waits for them, and re-layouts  0.6 us (2%)
    pallas_call x1, Pallas kernels, body(): pl.pallas_call(functools.partial(kernel, nr, nc, slots, sc, nrhs), out_sh...  27.6 us
    slice x1, local copies, waits for them, and re-layouts, body(): return (out[0].reshape(loads.shape), out[1].reshape(loads.shape))  0.6 us

profile of v5, /device:TPU:0, one launch (start us, length us, event | category | flops | bytes accessed | tf_op | source)
XLA Modules:
  0.0 28.8 jit_solution(6701995143015953087)
XLA Ops:
  0.6 27.6 %shard_map.77 = f32[2,8,128]{2,1,0:T(8,128)S(1)} custom-call(f32[8,128]{1,0:T(8,128)} %bitcast.10, f32[2,128]{1,0:T(2,128)} %bitcast.13, f32[2,16]{1,0:T(2,128)} %bitcast.14, s32[2,128]{1,0:T(2,128)} %bitcast.15, f32[2,128,128]{2,1,0:T(8,128)} %bitcast.8, f32[2,128,128]{2,1,0:T(8,128)} %bitcast.9), custom_call_target="tpu_custom_call" | custom-call | tf_op jit(solution)/shard_map/pallas_call | solution.py:578
  28.2 0.6 %fusion = (f32[1,8,128]{2,1,0:T(8,128)}, f32[1,8,128]{2,1,0:T(8,128)}) fusion(f32[2,8,128]{2,1,0:T(8,128)S(1)} %shard_map.77), kind=kLoop, calls=%fused_computation | loop fusion | bytes 16384 | tf_op jit(solution)/shard_map/slice | solution.py:615
